TPU v7x, 32 devices: a whole 2x2x4 slice. The times are simulated.
32 devices in a mesh: row: 8 (over z, core), col: 4 (over y, x).
Axes of the slice: x: 2, y: 2, z: 4, core: 2. Of those that a mesh axis runs over, the one named last changes fastest.
Arguments:
- right_sides: float32 [4, 1024, 4096], P(None, 'row', 'col'), may hold values from -6 to 6
- low_left: bfloat16 [6, 4096, 128], P(None, 'col'), may hold values from -0.25 to 0.25
- low_right: bfloat16 [6, 4096, 128], P(None, 'col'), may hold values from -0.09375 to 0.09375
- up_left: bfloat16 [6, 4096, 128], P(None, 'col'), may hold values from -0.25 to 0.25
- up_right: bfloat16 [6, 4096, 128], P(None, 'col'), may hold values from -0.09375 to 0.09375
- low_ranks: int32 [6], replicated, may hold values from 1 to 4
- up_ranks: int32 [6], replicated, may hold values from 1 to 4
- inv_lower: bfloat16 [4, 4096, 4096], P(None, 'col', 'row'), may hold values from -0.09375 to 0.09375
- inv_upper: bfloat16 [4, 4096, 4096], P(None, 'col', 'row'), may hold values from -0.09375 to 0.09375
Outputs:
- solution: float32 [4, 1024, 4096], P(None, 'row', 'col')
Inputs may be any that keep to these rules, and one draw needn't show every extreme that they name: `low_ranks`: factor columns beyond 32 times this value are padding with arbitrary values and must be masked out. `up_ranks`: factor columns beyond 32 times this value are padding with arbitrary values and must be masked out.
All inputs are finite; a program needn't handle non-finite values.
Results may differ from a plain program's by a relative error of at most 0.03.
Values may be sent and summed in bfloat16 or wider, within the bound.
A program may use at most 64 MiB of HBM per device.

v0:
```python
import functools

import jax
import jax.numpy as jnp
import numpy as np
from jax import lax
from jax.experimental import pallas as pl
from jax.experimental.pallas import tpu as pltpu
from jax.sharding import PartitionSpec as P

RBLK = 32


def rank_mask(ranks, pair_index, rank_cols):
    columns = jnp.arange(rank_cols, dtype=jnp.int32)
    return (columns[None, :] < RBLK * ranks[pair_index][:, None]).astype(jnp.float32)


def times_inverse(block, inverse):
    return lax.dot_general(
        block, inverse, (((1,), (1,)), ((), ())), preferred_element_type=jnp.float32
    )


def sum_terms(moved, inverse):
    return times_inverse(moved, inverse)


def shards(
    right_sides, low_left, low_right, up_left, up_right, low_ranks, up_ranks, inv_lower, inv_upper
):
    tile_count = right_sides.shape[0]
    rank_cols = low_left.shape[2]
    residual = right_sides
    forward = []
    for section in range(tile_count):
        rounded = residual[section].astype(jnp.bfloat16)
        whole = lax.all_gather(rounded, "col", axis=1, tiled=True)
        moved = lax.all_to_all(whole, "row", split_axis=1, concat_axis=0, tiled=True)
        solved = lax.psum_scatter(
            sum_terms(moved, inv_lower[section]).astype(jnp.bfloat16),
            "row",
            scatter_dimension=0,
            tiled=True,
        ).astype(jnp.float32)
        forward.append(solved)
        if section + 1 < tile_count:
            pair_index = np.array(
                [tile * (tile - 1) // 2 + section for tile in range(section + 1, tile_count)],
                dtype=np.int32,
            )
            projections = jnp.einsum(
                "nw,mwr->mnr",
                solved.astype(jnp.bfloat16),
                low_right[pair_index],
                preferred_element_type=jnp.float32,
            )
            leading = lax.psum(projections[:1].astype(jnp.bfloat16), "col").astype(jnp.float32)
            if section + 2 < tile_count:
                remaining = lax.psum(projections[1:].astype(jnp.bfloat16), "col").astype(
                    jnp.float32
                )
                summed = jnp.concatenate([leading, remaining], axis=0)
            else:
                summed = leading
            masked = (summed * rank_mask(low_ranks, pair_index, rank_cols)[:, None, :]).astype(
                jnp.bfloat16
            )
            update = jnp.einsum(
                "mnr,mwr->mnw", masked, low_left[pair_index], preferred_element_type=jnp.float32
            )
            residual = residual.at[section + 1 :].add(-update)
    state = jnp.stack(forward)
    solutions = [None] * tile_count
    for section in range(tile_count - 1, -1, -1):
        rounded = state[section].astype(jnp.bfloat16)
        whole = lax.all_gather(rounded, "col", axis=1, tiled=True)
        moved = lax.all_to_all(whole, "row", split_axis=1, concat_axis=0, tiled=True)
        solved = lax.psum_scatter(
            sum_terms(moved, inv_upper[section]).astype(jnp.bfloat16),
            "row",
            scatter_dimension=0,
            tiled=True,
        ).astype(jnp.float32)
        solutions[section] = solved
        if section > 0:
            pair_index = np.array(
                [section * (section - 1) // 2 + tile for tile in range(section)], dtype=np.int32
            )
            projections = jnp.einsum(
                "nw,mwr->mnr",
                solved.astype(jnp.bfloat16),
                up_right[pair_index],
                preferred_element_type=jnp.float32,
            )
            leading = lax.psum(projections[-1:].astype(jnp.bfloat16), "col").astype(jnp.float32)
            if section > 1:
                remaining = lax.psum(projections[:-1].astype(jnp.bfloat16), "col").astype(
                    jnp.float32
                )
                summed = jnp.concatenate([remaining, leading], axis=0)
            else:
                summed = leading
            masked = (summed * rank_mask(up_ranks, pair_index, rank_cols)[:, None, :]).astype(
                jnp.bfloat16
            )
            update = jnp.einsum(
                "mnr,mwr->mnw", masked, up_left[pair_index], preferred_element_type=jnp.float32
            )
            state = state.at[:section].add(-update)
    return jnp.stack(solutions)


MESH = pl.DeviceIdType.MESH
STREAMS = 4
LAG = {"start": 0, "spread": 0.7, "multiply": 1.4, "reduce": 1.65, "relay": 2.6, "finish": 3.5}
PERIOD = 4


def schedule(streams):
    order = []
    for stream in range(streams):
        for stage, lag in LAG.items():
            at = lag + stream * PERIOD / streams
            late = int(at // PERIOD)
            order.append((at - late * PERIOD, -late, stream, stage))
    return sorted(order)


def kernel(
    shape, rhs, low_left, low_right, up_left, up_right, masks, inv_lower, inv_upper, out,
    inv, left, right, source, moved, own, other, landed, chunks, arrived, proj, proj_in,
    load_sem, g1_send, g1_recv, g2_send, g2_recv, d_send, d_recv, r_send, r_recv, p_send, p_recv,
):
    tiles, rows, cols, chips, streams, part = shape
    pairs = low_left.shape[0]
    per_col = rows // cols
    lanes = inv_lower.shape[2]
    piece = lanes // cols
    row, col = lax.axis_index("row"), lax.axis_index("col")
    chip, core = lax.div(row, 2), lax.rem(row, 2)
    pair_at, member, pair_count = lax.div(chip, 2), lax.rem(chip, 2), chips // 2

    loads = [(rhs, out)]
    loads += [(inv_lower.at[k], inv.at[k]) for k in range(tiles)]
    loads += [(low_right, right.at[pl.ds(0, pairs)]), (low_left, left.at[pl.ds(0, pairs)])]
    loads += [(up_right, right.at[pl.ds(pairs, pairs)]), (up_left, left.at[pl.ds(pairs, pairs)])]
    loads += [(inv_upper.at[k], inv.at[2 * tiles - 1 - k]) for k in range(tiles - 1, -1, -1)]
    slots = [0] + list(range(1, 1 + tiles)) + [2 * tiles + 1 + k for k in range(4)]
    slots += list(range(1 + tiles, 1 + 2 * tiles))
    copies = [pltpu.make_async_copy(a, b, load_sem.at[s]) for (a, b), s in zip(loads, slots)]
    for copy in copies:
        copy.start()
    proj[...] = jnp.zeros_like(proj)
    copies[0].wait()

    def remote(src, dst, send, recv, to_row, to_col):
        return pltpu.make_async_remote_copy(
            src_ref=src, dst_ref=dst, send_sem=send, recv_sem=recv,
            device_id=(to_row, to_col), device_id_type=MESH,
        )

    def own_lanes():
        return pl.ds(pl.multiple_of(col * piece, piece), piece)

    def geometry(step):
        back = lax.div(step, tiles)
        section = step + back * (2 * tiles - 1 - 2 * step)
        count = (1 - back) * (tiles - 1 - section) + back * section
        return back, section, count

    def tile_of(back, section, u):
        tile = (1 - back) * (section + 1) + u
        pair = (1 - back) * (lax.div(tile * (tile + 2 * tiles - 1), 2) - tile * tiles + section)
        pair = pair + back * (pairs + lax.div(section * (section + 2 * tiles - 1), 2) - section * tiles + u)
        return tile, pair

    def place(stream):
        return pl.ds(stream * part, part)

    def g1(step, stream, half, q):
        side = lax.rem(step, 2)
        return remote(
            source.at[stream, :, pl.ds(half * lanes + q * piece, piece)],
            moved.at[side, stream, core, chip, :, pl.ds(q * piece, piece)],
            g1_send.at[stream, half * cols + q],
            g1_recv.at[stream, side, row],
            col * per_col + half,
            q,
        )

    def g1_mine(half, q):
        return jnp.logical_and(row == col * per_col + half, col == q)

    def g2(step, stream, hop):
        side = lax.rem(step, 2)
        view = moved.at[side, stream, :, :, :, own_lanes()]
        return remote(
            view, view, g2_send.at[stream, hop], g2_recv.at[stream, side, hop],
            row, lax.rem(col + hop, cols),
        )

    def swap(step, stream):
        side = lax.rem(step, 2)
        return remote(
            other.at[stream], landed.at[side, stream], d_send.at[stream], d_recv.at[stream, side],
            row + 1 - 2 * core, col,
        )

    def pass_on(step, stream, slot, to):
        side = lax.rem(step, 2)
        return remote(
            chunks.at[stream, slot], arrived.at[side, stream, slot],
            r_send.at[stream, slot], r_recv.at[stream, side, slot],
            2 * to + core, col,
        )

    def pair_copy(step, stream, hop):
        return pass_on(step, stream, hop, chip + 1 - 2 * member)

    def relay_copy(step, stream, hop):
        return pass_on(step, stream, pair_count + hop, 2 * lax.rem(pair_at + hop, pair_count) + member)

    def held_sum(step, stream, to):
        return own[stream, to] + landed[lax.rem(step, 2), stream, to].astype(jnp.float32)

    def project(step, stream, hop):
        side = lax.rem(step, 2)
        return remote(
            proj.at[stream], proj_in.at[side, stream, hop],
            p_send.at[stream, hop], p_recv.at[stream, side, hop],
            row, lax.rem(col + hop, cols),
        )

    def update(step, stream):
        back, section, count = geometry(step)
        side = lax.rem(step, 2)
        for hop in range(1, cols):
            project(step, stream, hop).wait()

        def one(u, carry):
            tile, pair = tile_of(back, section, u)
            total = proj[stream, u].astype(jnp.float32)
            for hop in range(1, cols):
                total += proj_in[side, stream, hop, u].astype(jnp.float32)
            masked = (total * masks[pair]).astype(jnp.bfloat16)
            out[tile, place(stream), :] -= times_inverse(masked, left[pair])
            return carry

        lax.fori_loop(0, count, one, 0)

    def start(step, stream):
        @pl.when(jnp.logical_and(step > 0, step != tiles))
        def _():
            update(step - 1, stream)

        _, section, _ = geometry(step)
        source[stream] = out[section, place(stream), :].astype(jnp.bfloat16)
        for half in range(per_col):
            for q in range(cols):
                copy = g1(step, stream, half, q)
                mine = g1_mine(half, q)

                @pl.when(jnp.logical_not(mine))
                def _():
                    copy.start()

                @pl.when(mine)
                def _():
                    pltpu.make_async_copy(
                        copy.src_ref, copy.dst_ref, g1_recv.at[stream, lax.rem(step, 2), row]
                    ).start()

    def spread(step, stream):
        side = lax.rem(step, 2)
        for k in range(rows):
            view = moved.at[side, stream, k % 2, k // 2, :, own_lanes()]
            pltpu.make_async_copy(view, view, g1_recv.at[stream, side, k]).wait()
        for hop in range(1, cols):
            g2(step, stream, hop).start()
        for half in range(per_col):
            for q in range(cols):

                @pl.when(jnp.logical_not(g1_mine(half, q)))
                def _():
                    g1(step, stream, half, q).wait_send()

    def multiply(step, stream):
        side = lax.rem(step, 2)
        if stream == 0:
            pltpu.make_async_copy(inv_lower.at[0], inv.at[step], load_sem.at[1 + step]).wait()
        for hop in range(1, cols):
            view = moved.at[
                side, stream, :, :, :,
                pl.ds(pl.multiple_of(lax.rem(col + cols - hop, cols) * piece, piece), piece),
            ]
            pltpu.make_async_copy(view, view, g2_recv.at[stream, side, hop]).wait()
        theirs = moved[side, stream, 1 - core].reshape(chips * part, lanes)
        other[stream] = (
            times_inverse(theirs, inv[step]).astype(jnp.bfloat16).reshape(chips, part, -1)
        )
        swap(step, stream).start()
        ours = moved[side, stream, core].reshape(chips * part, lanes)
        own[stream] = times_inverse(ours, inv[step]).reshape(chips, part, -1)
        for hop in range(1, cols):
            g2(step, stream, hop).wait_send()

    def reduce(step, stream):
        swap(step, stream).wait()
        for hop in list(range(1, pair_count)) + [0]:
            to = 2 * lax.rem(pair_at + hop, pair_count) + 1 - member
            chunks[stream, hop] = held_sum(step, stream, to).astype(jnp.bfloat16)
            pair_copy(step, stream, hop).start()

    def relay(step, stream):
        side = lax.rem(step, 2)
        for hop in range(1, pair_count):
            pair_copy(step, stream, hop).wait()
            to = 2 * lax.rem(pair_at + hop, pair_count) + member
            total = held_sum(step, stream, to) + arrived[side, stream, hop].astype(jnp.float32)
            chunks[stream, pair_count + hop] = total.astype(jnp.bfloat16)
            relay_copy(step, stream, hop).start()

    def finish(step, stream):
        side = lax.rem(step, 2)
        back, section, count = geometry(step)
        total = held_sum(step, stream, chip)
        pair_copy(step, stream, 0).wait()
        total += arrived[side, stream, 0].astype(jnp.float32)
        for hop in range(1, pair_count):
            relay_copy(step, stream, hop).wait()
            total += arrived[side, stream, pair_count + hop].astype(jnp.float32)
        out[section, place(stream), :] = total
        if stream == 0:

            @pl.when(step == 0)
            def _():
                for k in range(1 + tiles, 5 + tiles):
                    copies[k].wait()

        @pl.when(count > 0)
        def _():
            rounded = out[section, place(stream), :].astype(jnp.bfloat16)

            def one(u, carry):
                _, pair = tile_of(back, section, u)
                proj[stream, u] = jnp.dot(
                    rounded, right[pair], preferred_element_type=jnp.float32
                ).astype(jnp.bfloat16)
                return carry

            lax.fori_loop(0, count, one, 0)
            for hop in range(1, cols):
                project(step, stream, hop).start()

    stages = {
        "start": start, "spread": spread, "multiply": multiply, "reduce": reduce, "relay": relay,
        "finish": finish,
    }
    steps = 2 * tiles
    order = schedule(streams)
    latest = -min(shift for _, shift, _, _ in order)

    def body(turn, carry):
        for _, shift, stream, stage in order:
            step = turn + shift

            @pl.when(jnp.logical_and(step >= 0, step < steps))
            def _():
                stages[stage](step, stream)

        return carry

    lax.fori_loop(0, steps + latest, body, 0)


def fused(
    rows, cols, streams, right_sides, low_left, low_right, up_left, up_right, low_ranks, up_ranks,
    inv_lower, inv_upper,
):
    tiles, held, wide = right_sides.shape
    pairs, _, rank_cols = low_left.shape
    lanes = inv_lower.shape[2]
    chips = rows // 2
    part = held // streams
    masks = rank_mask(
        jnp.concatenate([low_ranks, up_ranks]), np.arange(2 * pairs), rank_cols
    ).reshape(2 * pairs, 1, rank_cols)
    half = jnp.bfloat16
    dma = pltpu.SemaphoreType.DMA
    scratch = [
        pltpu.VMEM((2 * tiles, wide, lanes), half),
        pltpu.VMEM((2 * pairs, wide, rank_cols), half),
        pltpu.VMEM((2 * pairs, wide, rank_cols), half),
        pltpu.VMEM((streams, part, wide), half),
        pltpu.VMEM((2, streams, 2, chips, part, lanes), half),
        pltpu.VMEM((streams, chips, part, wide), jnp.float32),
        pltpu.VMEM((streams, chips, part, wide), half),
        pltpu.VMEM((2, streams, chips, part, wide), half),
        pltpu.VMEM((streams, chips, part, wide), half),
        pltpu.VMEM((2, streams, chips, part, wide), half),
        pltpu.VMEM((streams, tiles - 1, part, rank_cols), half),
        pltpu.VMEM((2, streams, cols, tiles - 1, part, rank_cols), half),
        dma((2 * tiles + 5,)),
        dma((streams, rows)), dma((streams, 2, rows)),
        dma((streams, cols)), dma((streams, 2, cols)),
        dma((streams,)), dma((streams, 2)),
        dma((streams, chips)), dma((streams, 2, chips)),
        dma((streams, cols)), dma((streams, 2, cols)),
    ]
    anywhere = pl.BlockSpec(memory_space=pl.ANY)
    vmem = pl.BlockSpec(memory_space=pltpu.VMEM)
    return pl.pallas_call(
        functools.partial(kernel, (tiles, rows, cols, chips, streams, part)),
        out_shape=jax.ShapeDtypeStruct(right_sides.shape, jnp.float32),
        in_specs=[anywhere] * 5 + [vmem] + [anywhere] * 2,
        out_specs=vmem,
        scratch_shapes=scratch,
        compiler_params=pltpu.CompilerParams(
            has_side_effects=True, vmem_limit_bytes=60 * 1024 * 1024
        ),
    )(right_sides, low_left, low_right, up_left, up_right, masks, inv_lower, inv_upper)


def pick(mesh):
    rows, cols = mesh.shape["row"], mesh.shape["col"]

    def run(right_sides, *rest):
        held, lanes = right_sides.shape[1], rest[-1].shape[2]
        fits = rows % 4 == 0 and rows % cols == 0 and lanes % (128 * cols) == 0
        if fits and held % (16 * STREAMS) == 0:
            return fused(rows, cols, STREAMS, right_sides, *rest)
        return shards(right_sides, *rest)

    return run


def solution(mesh):
    in_specs = (
        P(None, "row", "col"),
        P(None, "col", None),
        P(None, "col", None),
        P(None, "col", None),
        P(None, "col", None),
        P(),
        P(),
        P(None, "col", "row"),
        P(None, "col", "row"),
    )
    out_specs = P(None, "row", "col")
    return jax.shard_map(pick(mesh), mesh=mesh, in_specs=in_specs, out_specs=out_specs, check_vma=False)
```

profile of v0, /device:TPU:0, one launch (start us, length us, event | category | flops | bytes accessed | tf_op | source)
XLA Modules:
  0.0 304.3 jit_solution(13526217055980984246)
XLA Ops:
  0.0 0.7 pad_add_fusion
  0.8 0.7 gather_fusion
  1.4 0.7 compare_convert_fusion.masks
  2.1 299.1 %shard_map.109 = f32[4,128,1024]{2,1,0:T(8,128)} custom-call(f32[4,128,1024]{2,1,0:T(8,128)} %rhs.1, bf16[6,1024,128]{2,1,0:T(8,128)(2,1)} %low_left.1, bf16[6,1024,128]{2,1,0:T(8,128)(2,1)} %low_right.1, bf16[6,1024,128]{2,1,0:T(8,128)(2,1)} %up_left.1, bf16[6,1024,128]{2,1,0:T(8,128)(2,1)} %up_right.1, f32[12,1,128]{2,1,0:T(1,128)} %compare_convert_fusion.masks, ...), custom_call_target="tpu_custom_call" | custom-call | tf_op jit(solution)/shard_map/pallas_call | solution.py:413
  301.2 3.2 %copy.13 = f32[4,128,1024]{2,1,0:T(8,128)} copy(f32[4,128,1024]{2,1,0:T(8,128)} %shard_map.109) | data formatting | bytes 4194304
  (3 shorter events, 0.0 us)
where the time goes:
time: 305 us; the launch traced here: 304 us
  Pallas kernels  299 us (98%)
  local copies, waits for them, and re-layouts  3.82 us (1%)
    pallas_call x1, Pallas kernels, fused(): pl.pallas_call(functools.partial(kernel, (tiles, rows, cols, chips, strea...  299 us

commit v1 on v0

v1 whole, which is shorter than its diff:
```python
import functools

import jax
import jax.numpy as jnp
import numpy as np
from jax import lax
from jax.experimental import pallas as pl
from jax.experimental.pallas import tpu as pltpu
from jax.sharding import PartitionSpec as P

RBLK = 32


def rank_mask(ranks, pair_index, rank_cols):
    columns = jnp.arange(rank_cols, dtype=jnp.int32)
    return (columns[None, :] < RBLK * ranks[pair_index][:, None]).astype(jnp.float32)


def times_inverse(block, inverse):
    return lax.dot_general(
        block, inverse, (((1,), (1,)), ((), ())), preferred_element_type=jnp.float32
    )


def sum_terms(moved, inverse):
    return times_inverse(moved, inverse)


def shards(
    right_sides, low_left, low_right, up_left, up_right, low_ranks, up_ranks, inv_lower, inv_upper
):
    tile_count = right_sides.shape[0]
    rank_cols = low_left.shape[2]
    residual = right_sides
    forward = []
    for section in range(tile_count):
        rounded = residual[section].astype(jnp.bfloat16)
        whole = lax.all_gather(rounded, "col", axis=1, tiled=True)
        moved = lax.all_to_all(whole, "row", split_axis=1, concat_axis=0, tiled=True)
        solved = lax.psum_scatter(
            sum_terms(moved, inv_lower[section]).astype(jnp.bfloat16),
            "row",
            scatter_dimension=0,
            tiled=True,
        ).astype(jnp.float32)
        forward.append(solved)
        if section + 1 < tile_count:
            pair_index = np.array(
                [tile * (tile - 1) // 2 + section for tile in range(section + 1, tile_count)],
                dtype=np.int32,
            )
            projections = jnp.einsum(
                "nw,mwr->mnr",
                solved.astype(jnp.bfloat16),
                low_right[pair_index],
                preferred_element_type=jnp.float32,
            )
            leading = lax.psum(projections[:1].astype(jnp.bfloat16), "col").astype(jnp.float32)
            if section + 2 < tile_count:
                remaining = lax.psum(projections[1:].astype(jnp.bfloat16), "col").astype(
                    jnp.float32
                )
                summed = jnp.concatenate([leading, remaining], axis=0)
            else:
                summed = leading
            masked = (summed * rank_mask(low_ranks, pair_index, rank_cols)[:, None, :]).astype(
                jnp.bfloat16
            )
            update = jnp.einsum(
                "mnr,mwr->mnw", masked, low_left[pair_index], preferred_element_type=jnp.float32
            )
            residual = residual.at[section + 1 :].add(-update)
    state = jnp.stack(forward)
    solutions = [None] * tile_count
    for section in range(tile_count - 1, -1, -1):
        rounded = state[section].astype(jnp.bfloat16)
        whole = lax.all_gather(rounded, "col", axis=1, tiled=True)
        moved = lax.all_to_all(whole, "row", split_axis=1, concat_axis=0, tiled=True)
        solved = lax.psum_scatter(
            sum_terms(moved, inv_upper[section]).astype(jnp.bfloat16),
            "row",
            scatter_dimension=0,
            tiled=True,
        ).astype(jnp.float32)
        solutions[section] = solved
        if section > 0:
            pair_index = np.array(
                [section * (section - 1) // 2 + tile for tile in range(section)], dtype=np.int32
            )
            projections = jnp.einsum(
                "nw,mwr->mnr",
                solved.astype(jnp.bfloat16),
                up_right[pair_index],
                preferred_element_type=jnp.float32,
            )
            leading = lax.psum(projections[-1:].astype(jnp.bfloat16), "col").astype(jnp.float32)
            if section > 1:
                remaining = lax.psum(projections[:-1].astype(jnp.bfloat16), "col").astype(
                    jnp.float32
                )
                summed = jnp.concatenate([remaining, leading], axis=0)
            else:
                summed = leading
            masked = (summed * rank_mask(up_ranks, pair_index, rank_cols)[:, None, :]).astype(
                jnp.bfloat16
            )
            update = jnp.einsum(
                "mnr,mwr->mnw", masked, up_left[pair_index], preferred_element_type=jnp.float32
            )
            state = state.at[:section].add(-update)
    return jnp.stack(solutions)


MESH = pl.DeviceIdType.MESH
STREAMS = 8
LAG = {"start": 0, "cross": 1.1, "spread": 3.1, "multiply": 5.2, "share": 6.6, "relay1": 7.6, "relay2": 9.6, "finish": 11.6, "late": 13.0}
TURN = 4


def schedule(streams, tiles):
    order = []
    for back in range(2):
        for stream in range(streams):
            for stage, lag in LAG.items():
                at = (lag + stream + back * TURN) / streams
                order.append((at - int(at), int(at), back, stream, stage))
    return sorted(order, key=lambda event: (event[0], -event[1]))


def kernel(
    shape, rhs, low_left, low_right, up_left, up_right, masks, inv_lower, inv_upper, out,
    inv, left, right, source, crossing, moved, own, chunks, arrived, near, near_in, proj, proj_in, far, far_in,
    rhs_sem, load_sem, factor_sem, w_send, w_recv, g0_send, g0_recv, g1_send, g1_recv, g2_send, g2_recv, r_send, r_recv,
    n_send, n_recv, p_send, p_recv, f_send, f_recv,
):
    tiles, rows, cols, chips, streams, part = shape
    pairs = low_left.shape[0]
    wide = out.shape[2]
    lanes = inv_lower.shape[2]
    piece = wide // cols
    row, col = lax.axis_index("row"), lax.axis_index("col")
    chip, core = lax.div(row, 2), lax.rem(row, 2)
    steps = 2 * tiles

    def remote(src, dst, send, recv, to_row, to_col):
        return pltpu.make_async_remote_copy(
            src_ref=src, dst_ref=dst, send_sem=send, recv_sem=recv,
            device_id=(to_row, to_col), device_id_type=MESH,
        )

    def inverse_of(step):
        return inv_lower.at[step] if step < tiles else inv_upper.at[steps - 1 - step]

    def half(step, which):
        return inv.at[step, :, pl.ds(pl.multiple_of(which * lanes, lanes), lanes)]

    def load_inverse(step):
        return pltpu.make_async_copy(inverse_of(step), half(step, core), load_sem.at[step])

    def lend_inverse(step):
        return remote(
            inverse_of(step), half(step, core), w_send.at[step], w_recv.at[step], row + 1 - 2 * core, col
        )

    factors = [
        (low_right, right.at[pl.ds(0, pairs)]), (low_left, left.at[pl.ds(0, pairs)]),
        (up_right, right.at[pl.ds(pairs, pairs)]), (up_left, left.at[pl.ds(pairs, pairs)]),
    ]
    factors = [pltpu.make_async_copy(a, b, factor_sem.at[k]) for k, (a, b) in enumerate(factors)]
    sides = [pltpu.make_async_copy(rhs.at[k], out.at[k], rhs_sem.at[k]) for k in range(tiles)]
    sides[0].start()
    for step in range(steps):
        lend_inverse(step).start()
        load_inverse(step).start()
        if step < tiles:
            factors[step].start()
            if step + 1 < tiles:
                sides[step + 1].start()
    far[...] = jnp.zeros_like(far)
    sides[0].wait()

    def own_lanes():
        return pl.ds(pl.multiple_of(col * piece, piece), piece)

    def geometry(step):
        back = lax.div(step, tiles)
        section = step + back * (2 * tiles - 1 - 2 * step)
        count = (1 - back) * (tiles - 1 - section) + back * section
        return back, section, count

    def tile_of(back, section, v):
        tile = section + (1 - 2 * back) * (1 + v)
        high = back * section + (1 - back) * tile
        low = section + tile - high
        return tile, back * pairs + lax.div(high * (high - 1), 2) + low

    def place(stream):
        return pl.ds(stream * part, part)

    def side_of(step):
        return lax.rem(step, 2)

    def g0(step, stream, hop):
        to = lax.rem(col + hop, cols)
        return remote(
            source.at[stream, :, pl.ds(pl.multiple_of(to * piece, piece), piece)],
            crossing.at[side_of(step), stream, col],
            g0_send.at[stream, hop], g0_recv.at[stream, side_of(step), col],
            row, to,
        )

    def g1(step, stream, hop):
        to = lax.rem(chip + hop, chips)
        return remote(
            crossing.at[side_of(step), stream, to],
            moved.at[side_of(step), stream, chip, :, own_lanes()],
            g1_send.at[stream, hop], g1_recv.at[stream, side_of(step), chip],
            2 * to + core, col,
        )

    def g2(step, stream, hop):
        view = moved.at[side_of(step), stream, :, :, own_lanes()]
        return remote(
            view, view, g2_send.at[stream, hop], g2_recv.at[stream, side_of(step), hop],
            row, lax.rem(col + hop, cols),
        )

    def pass_on(step, stream, owner, way):
        side = side_of(step)
        to = chip + way
        slot = owner + lax.div(1 - way, 2) * jnp.where(owner == to, chips - owner, 0)
        return remote(
            chunks.at[side, stream, owner], arrived.at[side, stream, slot],
            r_send.at[stream, side, owner], r_recv.at[stream, side, slot],
            2 * to + core, col,
        )

    def took(step, stream, slot):
        side = side_of(step)
        view = arrived.at[side, stream, slot]
        pltpu.make_async_copy(view, view, r_recv.at[stream, side, slot]).wait()
        return arrived[side, stream, slot].astype(jnp.float32)

    def line(step, stream, leg):
        side = side_of(step)
        up, down = chip == leg, chip == chips - 1 - leg

        @pl.when(jnp.logical_or(up, down))
        def _():
            way = jnp.where(up, 1, -1)

            def one(k, carry):
                owner = jnp.where(up, chips - 1 - k, k)
                total = own[side, stream, owner]
                if leg > 0:
                    total += took(step, stream, owner)
                chunks[side, stream, owner] = total.astype(jnp.bfloat16)
                pass_on(step, stream, owner, way).start()
                return carry

            lax.fori_loop(0, chips - 1 - leg, one, 0)

    def near_copy(step, stream, hop):
        to = lax.rem(chip + hop, chips)
        return remote(
            near.at[stream, to], near_in.at[side_of(step), stream, hop],
            n_send.at[stream, hop], n_recv.at[stream, side_of(step), hop],
            2 * to + core, col,
        )

    def project(step, stream, hop):
        return remote(
            proj.at[stream], proj_in.at[side_of(step), stream, hop],
            p_send.at[stream, hop], p_recv.at[stream, side_of(step), hop],
            row, lax.rem(col + hop, cols),
        )

    def project_far(step, stream, hop):
        return remote(
            far.at[stream], far_in.at[side_of(step), stream, hop],
            f_send.at[stream, hop], f_recv.at[stream, side_of(step), hop],
            row, lax.rem(col + hop, cols),
        )

    def subtract(tile, pair, stream, total):
        masked = (total * masks[pair]).astype(jnp.bfloat16)
        out[tile, place(stream), :] -= times_inverse(masked, left[pair])

    def start(step, stream):
        @pl.when(jnp.logical_and(step > 0, step != tiles))
        def _():
            if stream == 0:

                @pl.when(step == 1)
                def _():
                    for k in range(1, tiles):
                        sides[k].wait()
                    for k in range(1, 4):
                        factors[k].wait()

            back, section, _ = geometry(step - 1)
            tile, pair = tile_of(back, section, 0)
            for hop in range(1, cols):
                project(step - 1, stream, hop).wait()
            total = proj[stream].astype(jnp.float32)
            for hop in range(1, cols):
                total += proj_in[side_of(step - 1), stream, hop].astype(jnp.float32)
            subtract(tile, pair, stream, total)

        _, section, _ = geometry(step)
        source[stream] = out[section, place(stream), :].astype(jnp.bfloat16)
        mine = pl.ds(pl.multiple_of(col * piece, piece), piece)
        pltpu.make_async_copy(
            source.at[stream, :, mine], crossing.at[side_of(step), stream, col],
            g0_recv.at[stream, side_of(step), col],
        ).start()
        for hop in range(1, cols):
            g0(step, stream, hop).start()

    def cross(step, stream):
        side = side_of(step)
        for k in range(cols):
            view = crossing.at[side, stream, k]
            pltpu.make_async_copy(view, view, g0_recv.at[stream, side, k]).wait()
        pltpu.make_async_copy(
            crossing.at[side, stream, chip], moved.at[side, stream, chip, :, own_lanes()],
            g1_recv.at[stream, side, chip],
        ).start()
        for hop in range(1, chips):
            g1(step, stream, hop).start()
        for hop in range(1, cols):
            g0(step, stream, hop).wait_send()

    def spread(step, stream):
        for k in range(chips):
            view = moved.at[side_of(step), stream, k, :, own_lanes()]
            pltpu.make_async_copy(view, view, g1_recv.at[stream, side_of(step), k]).wait()
        for hop in range(1, cols):
            g2(step, stream, hop).start()
        for hop in range(1, chips):
            g1(step, stream, hop).wait_send()

    def multiply(step, stream):
        side = side_of(step)
        back, section, count = geometry(step)
        if stream == 0:
            view = half(step, core)
            pltpu.make_async_copy(view, view, load_sem.at[step]).wait()
            view = half(step, 1 - core)
            pltpu.make_async_copy(view, view, w_recv.at[step]).wait()

            @pl.when(step == 0)
            def _():
                factors[0].wait()

        for hop in range(1, cols):
            view = moved.at[
                side, stream, :, :,
                pl.ds(pl.multiple_of(lax.rem(col + cols - hop, cols) * piece, piece), piece),
            ]
            pltpu.make_async_copy(view, view, g2_recv.at[stream, side, hop]).wait()
        whole = moved[side, stream].reshape(chips * part, wide)
        terms = times_inverse(whole, inv[step])
        own[side, stream] = terms.reshape(chips, part, wide)

        @pl.when(count > 0)
        def _():
            _, pair = tile_of(back, section, 0)
            rounded = own[side, stream].reshape(chips * part, wide).astype(jnp.bfloat16)
            near[stream] = (
                jnp.dot(rounded, right[pair], preferred_element_type=jnp.float32)
                .astype(jnp.bfloat16)
                .reshape(chips, part, -1)
            )
            for hop in range(1, chips):
                near_copy(step, stream, hop).start()

        line(step, stream, 0)
        for hop in range(1, cols):
            g2(step, stream, hop).wait_send()

    def share(step, stream):
        _, _, count = geometry(step)

        @pl.when(count > 0)
        def _():
            for hop in range(1, chips):
                near_copy(step, stream, hop).wait()
            total = near[stream, chip].astype(jnp.float32)
            for hop in range(1, chips):
                total += near_in[side_of(step), stream, hop].astype(jnp.float32)
            proj[stream] = total.astype(jnp.bfloat16)
            for hop in range(1, cols):
                project(step, stream, hop).start()

    def finish(step, stream):
        side = side_of(step)
        back, section, count = geometry(step)
        out[section, place(stream), :] = own[side, stream, chip]

        @pl.when(chip > 0)
        def _():
            out[section, place(stream), :] += took(step, stream, chip)

        @pl.when(chip < chips - 1)
        def _():
            out[section, place(stream), :] += took(step, stream, chips)

        for owner in range(chips):

            @pl.when(chip != owner)
            def _():
                pass_on(step, stream, owner, jnp.where(owner > chip, 1, -1)).wait_send()

        @pl.when(count > 1)
        def _():
            rounded = out[section, place(stream), :].astype(jnp.bfloat16)

            def one(v, carry):
                _, pair = tile_of(back, section, v)
                far[stream, v - 1] = jnp.dot(
                    rounded, right[pair], preferred_element_type=jnp.float32
                ).astype(jnp.bfloat16)
                return carry

            lax.fori_loop(1, count, one, 0)
            for hop in range(1, cols):
                project_far(step, stream, hop).start()

    def late(step, stream):
        back, section, count = geometry(step)
        side = side_of(step)

        @pl.when(count > 1)
        def _():
            for hop in range(1, cols):
                project_far(step, stream, hop).wait()

            def one(v, carry):
                tile, pair = tile_of(back, section, v)
                total = far[stream, v - 1].astype(jnp.float32)
                for hop in range(1, cols):
                    total += far_in[side, stream, hop, v - 1].astype(jnp.float32)
                subtract(tile, pair, stream, total)
                return carry

            lax.fori_loop(1, count, one, 0)

    stages = {
        "start": start, "cross": cross, "spread": spread, "multiply": multiply, "share": share,
        "relay1": functools.partial(line, leg=1), "relay2": functools.partial(line, leg=2),
        "finish": finish, "late": late,
    }
    order = schedule(streams, tiles)
    latest = max(shift for _, shift, _, _, _ in order)

    def body(turn, carry):
        for _, shift, back, stream, stage in order:
            step = turn - shift

            @pl.when(jnp.logical_and(step >= back * tiles, step < (1 + back) * tiles))
            def _():
                stages[stage](step, stream)

        return carry

    lax.fori_loop(0, steps + latest, body, 0)
    for step in range(steps):
        lend_inverse(step).wait_send()


def fused(
    rows, cols, streams, right_sides, low_left, low_right, up_left, up_right, low_ranks, up_ranks,
    inv_lower, inv_upper,
):
    tiles, held, wide = right_sides.shape
    pairs, _, rank_cols = low_left.shape
    chips = rows // 2
    part = held // streams
    masks = rank_mask(
        jnp.concatenate([low_ranks, up_ranks]), np.arange(2 * pairs), rank_cols
    ).reshape(2 * pairs, 1, rank_cols)
    half = jnp.bfloat16
    dma = pltpu.SemaphoreType.DMA
    later = max(tiles - 2, 1)
    scratch = [
        pltpu.VMEM((2 * tiles, wide, wide), half),
        pltpu.VMEM((2 * pairs, wide, rank_cols), half),
        pltpu.VMEM((2 * pairs, wide, rank_cols), half),
        pltpu.VMEM((streams, part, wide), half),
        pltpu.VMEM((2, streams, cols, part, wide // cols), half),
        pltpu.VMEM((2, streams, chips, part, wide), half),
        pltpu.VMEM((2, streams, chips, part, wide), jnp.float32),
        pltpu.VMEM((2, streams, chips, part, wide), half),
        pltpu.VMEM((2, streams, chips + 1, part, wide), half),
        pltpu.VMEM((streams, chips, part, rank_cols), half),
        pltpu.VMEM((2, streams, chips, part, rank_cols), half),
        pltpu.VMEM((streams, part, rank_cols), half),
        pltpu.VMEM((2, streams, cols, part, rank_cols), half),
        pltpu.VMEM((streams, later, part, rank_cols), half),
        pltpu.VMEM((2, streams, cols, later, part, rank_cols), half),
        dma((tiles,)), dma((2 * tiles,)), dma((4,)), dma((2 * tiles,)), dma((2 * tiles,)),
        dma((streams, cols)), dma((streams, 2, cols)),
        dma((streams, chips)), dma((streams, 2, chips)),
        dma((streams, cols)), dma((streams, 2, cols)),
        dma((streams, 2, chips)), dma((streams, 2, chips + 1)),
        dma((streams, chips)), dma((streams, 2, chips)),
        dma((streams, cols)), dma((streams, 2, cols)),
        dma((streams, cols)), dma((streams, 2, cols)),
    ]
    anywhere = pl.BlockSpec(memory_space=pl.ANY)
    vmem = pl.BlockSpec(memory_space=pltpu.VMEM)
    return pl.pallas_call(
        functools.partial(kernel, (tiles, rows, cols, chips, streams, part)),
        out_shape=jax.ShapeDtypeStruct(right_sides.shape, jnp.float32),
        in_specs=[anywhere] * 5 + [vmem] + [anywhere] * 2,
        out_specs=vmem,
        scratch_shapes=scratch,
        compiler_params=pltpu.CompilerParams(
            has_side_effects=True, vmem_limit_bytes=60 * 1024 * 1024
        ),
    )(right_sides, low_left, low_right, up_left, up_right, masks, inv_lower, inv_upper)


def pick(mesh):
    rows, cols = mesh.shape["row"], mesh.shape["col"]

    def run(right_sides, *rest):
        tiles, held, wide = right_sides.shape
        fits = rows == 8 and cols == 4 and tiles == 4 and wide == 2 * rest[-1].shape[2]
        if fits and wide % (128 * cols) == 0 and held % (16 * STREAMS) == 0:
            return fused(rows, cols, STREAMS, right_sides, *rest)
        return shards(right_sides, *rest)

    return run


def solution(mesh):
    in_specs = (
        P(None, "row", "col"),
        P(None, "col", None),
        P(None, "col", None),
        P(None, "col", None),
        P(None, "col", None),
        P(),
        P(),
        P(None, "col", "row"),
        P(None, "col", "row"),
    )
    out_specs = P(None, "row", "col")
    return jax.shard_map(pick(mesh), mesh=mesh, in_specs=in_specs, out_specs=out_specs, check_vma=False)
```

time: 305 us -> 228 us (0.75)
  Pallas kernels: 299 us -> 222 us
    pallas_call x1, Pallas kernels: 299 us -> 222 us  [fused(): pl.pallas_call(functools.partial(kernel, (tiles, rows, cols, chips, strea...]
where the time goes in v1:
time: 228 us; the launch traced here: 227 us
  Pallas kernels  222 us (97%)
  local copies, waits for them, and re-layouts  3.82 us (2%)
    pallas_call x1, Pallas kernels, fused(): pl.pallas_call(functools.partial(kernel, (tiles, rows, cols, chips, strea...  222 us

profile of v1, /device:TPU:0, one launch (start us, length us, event | category | flops | bytes accessed | tf_op | source)
XLA Modules:
  0.0 227.3 jit_solution(6517584566509992928)
XLA Ops:
  0.0 0.7 pad_add_fusion
  0.8 0.7 gather_fusion
  1.4 0.7 compare_convert_fusion.masks
  2.1 222.0 %shard_map.109 = f32[4,128,1024]{2,1,0:T(8,128)} custom-call(f32[4,128,1024]{2,1,0:T(8,128)} %rhs.1, bf16[6,1024,128]{2,1,0:T(8,128)(2,1)} %low_left.1, bf16[6,1024,128]{2,1,0:T(8,128)(2,1)} %low_right.1, bf16[6,1024,128]{2,1,0:T(8,128)(2,1)} %up_left.1, bf16[6,1024,128]{2,1,0:T(8,128)(2,1)} %up_right.1, f32[12,1,128]{2,1,0:T(1,128)} %compare_convert_fusion.masks, ...), custom_call_target="tpu_custom_call" | custom-call | tf_op jit(solution)/shard_map/pallas_call | solution.py:513
  224.1 3.2 %copy.13 = f32[4,128,1024]{2,1,0:T(8,128)} copy(f32[4,128,1024]{2,1,0:T(8,128)} %shard_map.109) | data formatting | bytes 4194304
  (3 shorter events, 0.0 us)

commit v2 on v1

--- a/solution.py
+++ b/solution.py
@@ -113,17 +113,22 @@
 
 MESH = pl.DeviceIdType.MESH
 STREAMS = 8
-LAG = {"start": 0, "cross": 1.1, "spread": 3.1, "multiply": 5.2, "share": 6.6, "relay1": 7.6, "relay2": 9.6, "finish": 11.6, "late": 13.0}
-TURN = 4
+LAG = {"start": 0, "cross": 1.1, "spread": 3.1, "multiply": 4.6, "share": 6.3, "relay1": 7.3, "relay2": 9.1, "finish": 10.4, "late": 14.3}
+LAST = {"relay1": 6.6, "relay2": 7.8, "finish": 8.9}
+TURN = 1.0
 
 
 def schedule(streams, tiles):
     order = []
     for back in range(2):
         for stream in range(streams):
-            for stage, lag in LAG.items():
+            spans = [(stage, lag, 0, tiles - (stage in LAST)) for stage, lag in LAG.items()]
+            spans += [(stage, lag, tiles - 1, tiles) for stage, lag in LAST.items()]
+            for stage, lag, first, end in spans:
                 at = (lag + stream + back * TURN) / streams
-                order.append((at - int(at), int(at), back, stream, stage))
+                order.append(
+                    (at - int(at), int(at), back * tiles + first, back * tiles + end, stream, stage)
+                )
     return sorted(order, key=lambda event: (event[0], -event[1]))
 
 
@@ -452,13 +457,13 @@
         "finish": finish, "late": late,
     }
     order = schedule(streams, tiles)
-    latest = max(shift for _, shift, _, _, _ in order)
+    latest = max(event[1] for event in order)
 
     def body(turn, carry):
-        for _, shift, back, stream, stage in order:
+        for _, shift, first, end, stream, stage in order:
             step = turn - shift
 
-            @pl.when(jnp.logical_and(step >= back * tiles, step < (1 + back) * tiles))
+            @pl.when(jnp.logical_and(step >= first, step < end))
             def _():
                 stages[stage](step, stream)
 

time: 228 us -> 226 us (level)
  no operation moved by 1% of the time
where the time goes in v2:
time: 226 us
  Pallas kernels  220 us (97%)
  local copies, waits for them, and re-layouts  3.82 us (2%)
    pallas_call x1, Pallas kernels, fused(): pl.pallas_call(functools.partial(kernel, (tiles, rows, cols, chips, strea...  220 us

profile of v2, /device:TPU:0, one launch (start us, length us, event | category | flops | bytes accessed | tf_op | source)
XLA Modules:
  0.0 225.7 jit_solution(17796982950799797403)
XLA Ops:
  0.0 0.7 pad_add_fusion
  0.8 0.7 gather_fusion
  1.4 0.7 compare_convert_fusion.masks
  2.1 220.4 %shard_map.109 = f32[4,128,1024]{2,1,0:T(8,128)} custom-call(f32[4,128,1024]{2,1,0:T(8,128)} %rhs.1, bf16[6,1024,128]{2,1,0:T(8,128)(2,1)} %low_left.1, bf16[6,1024,128]{2,1,0:T(8,128)(2,1)} %low_right.1, bf16[6,1024,128]{2,1,0:T(8,128)(2,1)} %up_left.1, bf16[6,1024,128]{2,1,0:T(8,128)(2,1)} %up_right.1, f32[12,1,128]{2,1,0:T(1,128)} %compare_convert_fusion.masks, ...), custom_call_target="tpu_custom_call" | custom-call | tf_op jit(solution)/shard_map/pallas_call | solution.py:518
  222.5 3.2 %copy.13 = f32[4,128,1024]{2,1,0:T(8,128)} copy(f32[4,128,1024]{2,1,0:T(8,128)} %shard_map.109) | data formatting | bytes 4194304
  (3 shorter events, 0.0 us)

commit v3 on v2

--- a/solution.py
+++ b/solution.py
@@ -314,25 +314,24 @@
 
         _, section, _ = geometry(step)
         source[stream] = out[section, place(stream), :].astype(jnp.bfloat16)
-        mine = pl.ds(pl.multiple_of(col * piece, piece), piece)
+        for hop in range(1, cols):
+            g0(step, stream, hop).start()
         pltpu.make_async_copy(
-            source.at[stream, :, mine], crossing.at[side_of(step), stream, col],
+            source.at[stream, :, own_lanes()], crossing.at[side_of(step), stream, col],
             g0_recv.at[stream, side_of(step), col],
         ).start()
-        for hop in range(1, cols):
-            g0(step, stream, hop).start()
 
     def cross(step, stream):
         side = side_of(step)
         for k in range(cols):
             view = crossing.at[side, stream, k]
             pltpu.make_async_copy(view, view, g0_recv.at[stream, side, k]).wait()
+        for hop in range(1, chips):
+            g1(step, stream, hop).start()
         pltpu.make_async_copy(
             crossing.at[side, stream, chip], moved.at[side, stream, chip, :, own_lanes()],
             g1_recv.at[stream, side, chip],
         ).start()
-        for hop in range(1, chips):
-            g1(step, stream, hop).start()
         for hop in range(1, cols):
             g0(step, stream, hop).wait_send()
 

time: 226 us -> 226 us (level)
  no operation moved by 1% of the time
where the time goes in v3:
time: 226 us
  Pallas kernels  220 us (97%)
  local copies, waits for them, and re-layouts  3.82 us (2%)
    pallas_call x1, Pallas kernels, fused(): pl.pallas_call(functools.partial(kernel, (tiles, rows, cols, chips, strea...  220 us

profile of v3, /device:TPU:0, one launch (start us, length us, event | category | flops | bytes accessed | tf_op | source)
XLA Modules:
  0.0 225.5 jit_solution(14088549802736282945)
XLA Ops:
  0.0 0.7 pad_add_fusion
  0.8 0.7 gather_fusion
  1.4 0.7 compare_convert_fusion.masks
  2.1 220.3 %shard_map.109 = f32[4,128,1024]{2,1,0:T(8,128)} custom-call(f32[4,128,1024]{2,1,0:T(8,128)} %rhs.1, bf16[6,1024,128]{2,1,0:T(8,128)(2,1)} %low_left.1, bf16[6,1024,128]{2,1,0:T(8,128)(2,1)} %low_right.1, bf16[6,1024,128]{2,1,0:T(8,128)(2,1)} %up_left.1, bf16[6,1024,128]{2,1,0:T(8,128)(2,1)} %up_right.1, f32[12,1,128]{2,1,0:T(1,128)} %compare_convert_fusion.masks, ...), custom_call_target="tpu_custom_call" | custom-call | tf_op jit(solution)/shard_map/pallas_call | solution.py:517
  222.4 3.2 %copy.13 = f32[4,128,1024]{2,1,0:T(8,128)} copy(f32[4,128,1024]{2,1,0:T(8,128)} %shard_map.109) | data formatting | bytes 4194304
  (3 shorter events, 0.0 us)
